TPU v7x, 32 devices: a whole 2x2x4 slice. The times are simulated.
32 devices in a mesh: seq: 8 (over z, y), chan: 4 (over x, core).
Axes of the slice: x: 2, y: 2, z: 4, core: 2. Of those that a mesh axis runs over, the one named last changes fastest.
Arguments:
- inputs: float32 [1024, 8192], P('seq', 'chan'), may hold values from -6 to 6
- conv_weight: float32 [3, 4, 8192], P(None, None, 'chan'), may hold values from -3 to 3
- conv_bias: float32 [3, 8192], P(None, 'chan'), may hold values from -1 to 1
- cotangent: float32 [1024, 8192], P('seq', 'chan'), may hold values from -6 to 6
Outputs:
- output: float32 [1024, 8192], P('seq', 'chan')
- input_grad: float32 [1024, 8192], P('seq', 'chan')
- weight_grad: float32 [3, 4, 8192], P(None, None, 'chan')
- bias_grad: float32 [3, 8192], P(None, 'chan')
All inputs are finite; a program needn't handle non-finite values.
Results may differ from a plain program's by a relative error of at most 0.0001.
Values sent between devices are 32-bit elements; how exact they have to be, the bound alone decides.
No kernel may reach another device: no remote copies, remote signals or barrier semaphores. Data moves between devices by JAX's collectives and lax.ppermute only.
A program may use at most 64 MiB of HBM per device.

v0:
```python
import jax
import jax.numpy as jnp
from jax import lax
from jax.sharding import PartitionSpec as P


def passed_along(array, axis, by):
    devices = lax.axis_size(axis)
    pairs = [(i, i + by) for i in range(devices) if 0 <= i + by < devices]
    return lax.ppermute(array, axis, pairs)


def shards(inputs, conv_weight, conv_bias, cotangent):
    shard_len = inputs.shape[0]
    layers = conv_weight.shape[0]
    taps = conv_weight.shape[1]
    act = inputs
    saved = []
    for layer in range(layers):
        before = passed_along(act[shard_len - (taps - 1) :], "seq", 1)
        padded = jnp.concatenate([before, act], axis=0)
        preact = conv_bias[layer][None, :] + sum(
            (
                conv_weight[layer, offset][None, :] * padded[offset : offset + shard_len]
                for offset in range(taps)
            )
        )
        saved.append((padded, preact))
        act = preact * jax.nn.sigmoid(preact)
    grad = cotangent
    term_list = [None] * layers
    for layer in reversed(range(layers)):
        padded, preact = saved[layer]
        gate_value = jax.nn.sigmoid(preact)
        pre_grad = grad * gate_value * (1.0 + preact * (1.0 - gate_value))
        after = passed_along(pre_grad[: taps - 1], "seq", -1)
        grad_pad = jnp.concatenate([pre_grad, after], axis=0)
        grad = sum(
            (
                conv_weight[layer, offset][None, :]
                * grad_pad[taps - 1 - offset : taps - 1 - offset + shard_len]
                for offset in range(taps)
            )
        )
        weight_terms = [
            jnp.sum(pre_grad * padded[offset : offset + shard_len], axis=0)
            for offset in range(taps)
        ]
        term_list[layer] = jnp.stack(weight_terms + [jnp.sum(pre_grad, axis=0)])
    all_terms = jnp.stack(term_list)
    summed = lax.psum(all_terms, "seq")
    return (act, grad, summed[:, :taps], summed[:, taps])


def solution(mesh):
    in_specs = (P("seq", "chan"), P(None, None, "chan"), P(None, "chan"), P("seq", "chan"))
    out_specs = (P("seq", "chan"), P("seq", "chan"), P(None, None, "chan"), P(None, "chan"))
    return jax.shard_map(shards, mesh=mesh, in_specs=in_specs, out_specs=out_specs, check_vma=False)
```

profile of v0, /device:TPU:0, one launch (start us, length us, event | category | flops | bytes accessed | tf_op | source)
XLA Modules:
  0.0 137.0 jit_solution(2371675134209580371)
XLA Ops:
  7.2 0.0 all-reduce.2.cloned.1.call-start
  7.2 0.9 slice.150
  8.1 4.9 %collective-permute-start = (f32[3,2048]{1,0:T(4,128)S(1)}, f32[3,2048]{1,0:T(4,128)S(1)}, u32[]{:S(2)}, u32[]{:S(2)}) collective-permute-start(f32[3,2048]{1,0:T(4,128)S(1)} %slice.150), channel_id=1, source_target_pairs={{0,4},{4,8},{8,12},{12,16},{16,20},{20,24},{24,28},{1,5},{5,9},{9,... | collective-permute-start | bytes 73736 | tf_op jit(solution)/shard_map/ppermute | solution.py:10
  13.0 1.1 fusion.41
  14.1 0.9 fusion.42
  15.0 0.0 collective-permute-done
  15.0 3.4 %fusion.36 = (f32[128,2048]{1,0:T(8,128)S(1)}, f32[128,2048]{1,0:T(8,128)S(1)}) fusion(f32[128,2048]{1,0:T(8,128)} %param.4, f32[2048]{0:T(1024)S(1)} %bitcast.32, f32[3,2048]{1,0:T(4,128)S(1)} %collective-permute-done, f32[2048]{0:T(1024)S(1)} %bitcast.34, f32[2048]{0:T(1024)S(1)} %bitcast.36, f32[2048]{0:T(1024)S(1)} %bitcast.38, f32[2048]{0:T(1024)S(1)} %bitcast.58), kind=kLoop, calls=%fused_computation.84 | loop fusion | flops 3932160 | bytes 3211264 | tf_op jit(solution)/shard_map/mul | solution.py:29
  18.4 3.8 %collective-permute-start.1 = (f32[3,2048]{1,0:T(4,128)S(1)}, f32[3,2048]{1,0:T(4,128)S(1)}, u32[]{:S(2)}, u32[]{:S(2)}) collective-permute-start(f32[3,2048]{1,0:T(4,128)S(1)} %slice.189), channel_id=1, source_target_pairs={{0,4},{4,8},{8,12},{12,16},{16,20},{20,24},{24,28},{1,5},{5,9},{9,... | collective-permute-start | bytes 73736 | tf_op jit(solution)/shard_map/ppermute | solution.py:10
  22.2 1.6 %collective-permute-done.1 = f32[3,2048]{1,0:T(4,128)S(1)} collective-permute-done((f32[3,2048]{1,0:T(4,128)S(1)}, f32[3,2048]{1,0:T(4,128)S(1)}, u32[]{:S(2)}, u32[]{:S(2)}) %collective-permute-start.1) | collective-permute-done | bytes 24608 | tf_op jit(solution)/shard_map/ppermute | solution.py:10
  23.8 0.0 copy-start.2
  23.8 0.7 fusion.35
  24.5 4.3 %collective-permute-start.2 = (f32[3,2048]{1,0:T(4,128)S(1)}, f32[3,2048]{1,0:T(4,128)S(1)}, u32[]{:S(2)}, u32[]{:S(2)}) collective-permute-start(f32[3,2048]{1,0:T(4,128)S(1)} %slice.194), channel_id=1, source_target_pairs={{0,4},{4,8},{8,12},{12,16},{16,20},{20,24},{24,28},{1,5},{5,9},{9,... | collective-permute-start | bytes 73736 | tf_op jit(solution)/shard_map/ppermute | solution.py:10
  28.8 1.6 %collective-permute-done.2 = f32[3,2048]{1,0:T(4,128)S(1)} collective-permute-done((f32[3,2048]{1,0:T(4,128)S(1)}, f32[3,2048]{1,0:T(4,128)S(1)}, u32[]{:S(2)}, u32[]{:S(2)}) %collective-permute-start.2) | collective-permute-done | bytes 24608 | tf_op jit(solution)/shard_map/ppermute | solution.py:10
  30.4 0.0 copy-done.2
  30.4 1.5 %fusion.38 = (f32[2048]{0:T(1024)S(1)}, f32[2048]{0:T(1024)S(1)}, f32[2048]{0:T(1024)S(1)}, f32[2048]{0:T(1024)S(1)}, f32[2048]{0:T(1024)S(1)}, /*index=5*/f32[128,2048]{1,0:T(8,128)S(1)}, f32[128,2048]{1,0:T(8,128)S(1)}) fusion(f32[128,2048]{1,0:T(8,128)S(1)} %get-tuple-element.34, f32[128,2048]{1,0:T(8,128)S(1)} %get-tuple-element.33, ...), kind=kLoop, calls=%fused_computation.89 | loop fusion | flops 8902656 | bytes 5349376 | tf_op jit(solution)/shard_map/reduce_sum | solution.py:49
  31.9 1.3 collective-permute-start.3
  33.2 5.7 %collective-permute-done.3 = f32[3,2048]{1,0:T(4,128)S(1)} collective-permute-done((f32[3,2048]{1,0:T(4,128)S(1)}, f32[3,2048]{1,0:T(4,128)S(1)}, u32[]{:S(2)}, u32[]{:S(2)}) %collective-permute-start.3) | collective-permute-done | bytes 24608 | tf_op jit(solution)/shard_map/ppermute | solution.py:10
  38.9 1.7 %fusion.37 = (f32[2048]{0:T(1024)S(1)}, f32[2048]{0:T(1024)S(1)}, f32[2048]{0:T(1024)S(1)}, f32[2048]{0:T(1024)S(1)}, f32[2048]{0:T(1024)S(1)}, /*index=5*/f32[128,2048]{1,0:T(8,128)S(1)}) fusion(f32[128,2048]{1,0:T(8,128)S(1)} %get-tuple-element.36, f32[128,2048]{1,0:T(8,128)S(1)} %get-tuple-element.35, f32[3,2048]{1,0:T(4,128)S(1)} %collective-permute-done.1, ...), kind=kLoop, calls=%fused_computation.88 | loop fusion | flops 8902656 | bytes 5365760 | tf_op jit(solution)/shard_map/reduce_sum | solution.py:49
  40.6 0.0 copy-start.1
  40.6 1.3 collective-permute-start.4
  41.9 0.0 copy-start
  41.9 1.3 fusion.34
  43.2 0.0 copy-done.1
  43.2 0.1 stack.85
  43.3 0.1 stack.78
  43.4 4.2 %collective-permute-done.4 = f32[3,2048]{1,0:T(4,128)S(1)} collective-permute-done((f32[3,2048]{1,0:T(4,128)S(1)}, f32[3,2048]{1,0:T(4,128)S(1)}, u32[]{:S(2)}, u32[]{:S(2)}) %collective-permute-start.4) | collective-permute-done | bytes 24608 | tf_op jit(solution)/shard_map/ppermute | solution.py:10
  47.6 0.0 copy-done
  47.7 3.3 %multiply_reduce_fusion.9 = (f32[2048]{0:T(1024)S(1)}, f32[2048]{0:T(1024)S(1)}, f32[2048]{0:T(1024)S(1)}, f32[2048]{0:T(1024)S(1)}, f32[2048]{0:T(1024)S(1)}, /*index=5*/f32[128,2048]{1,0:T(8,128)S(1)}) fusion(f32[128,2048]{1,0:T(8,128)S(1)} %copy-done, f32[3,2048]{1,0:T(4,128)S(1)} %collective-permute-done, f32[128,2048]{1,0:T(8,128)S(1)} %get-tuple-element.36, ...), kind=kLoop, calls=%fused_computation.73 | loop fusion | flops 7854080 | bytes 4317184 | tf_op jit(solution)/shard_map/reduce_sum | solution.py:46
  51.0 0.1 stack.71
  51.1 1.3 collective-permute-start.5
  52.4 0.8 pad_maximum_fusion.6
  53.2 0.0 all-reduce.2.cloned.1.call-update
  53.2 4.6 %collective-permute-done.5 = f32[3,2048]{1,0:T(4,128)S(1)} collective-permute-done((f32[3,2048]{1,0:T(4,128)S(1)}, f32[3,2048]{1,0:T(4,128)S(1)}, u32[]{:S(2)}, u32[]{:S(2)}) %collective-permute-start.5) | collective-permute-done | bytes 24608 | tf_op jit(solution)/shard_map/ppermute | solution.py:10
  57.8 1.4 %fusion.4 = f32[128,2048]{1,0:T(8,128)} fusion(f32[128,2048]{1,0:T(8,128)S(1)} %get-tuple-element.29, f32[3,2048]{1,0:T(4,128)S(1)} %collective-permute-done.5, f32[2048]{0:T(1024)S(1)} %bitcast.33, f32[2048]{0:T(1024)S(1)} %bitcast.35, f32[2048]{0:T(1024)S(1)} %bitcast.37, f32[2048]{0:T(1024)S(1)} %bitcast.39), kind=kLoop, calls=%fused_computation.28 | loop fusion | flops 2621440 | bytes 2154496 | tf_op jit(solution)/shard_map/add | solution.py:38
  59.3 67.9 %all-reduce.2.cloned.1.call-done = f32[3,5,2048]{2,0,1:T(4,128)} async-done(((f32[3,5,2048]{2,0,1:T(4,128)}), f32[3,5,2048]{2,0,1:T(4,128)}) %all-reduce.2.cloned.1.call-update) | async-done | bytes 122896 | tf_op jit(solution)/shard_map/psum | solution.py:51
  127.1 0.9 slice.214
  128.1 0.7 copy.8
  128.8 1.4 %slice_bitcast_fusion = f32[3,2048]{1,0:T(4,128)} fusion(f32[3,5,2048]{2,0,1:T(4,128)} %all-reduce.2.cloned.1.call-done), kind=kLoop, calls=%fused_computation.87 | loop fusion | bytes 49152 | tf_op jit(solution)/shard_map/squeeze | solution.py:52
  (8 shorter events, 0.1 us)
Async XLA Ops:
  7.2 120.0 %all-reduce.2.cloned.1.call-start = ((), (), s32[]{:S(2)}) async-start(), calls=%async_computation | async-start | bytes 327680 | tf_op jit(solution)/shard_map/psum | solution.py:51
  8.1 6.9 %collective-permute-start = (f32[3,2048]{1,0:T(4,128)S(1)}, f32[3,2048]{1,0:T(4,128)S(1)}, u32[]{:S(2)}, u32[]{:S(2)}) collective-permute-start(f32[3,2048]{1,0:T(4,128)S(1)} %slice.150), channel_id=1, source_target_pairs={{0,4},{4,8},{8,12},{12,16},{16,20},{20,24},{24,28},{1,5},{5,9},{9,... | collective-permute-start | bytes 73736 | tf_op jit(solution)/shard_map/ppermute | solution.py:10
  18.4 5.4 %collective-permute-start.1 = (f32[3,2048]{1,0:T(4,128)S(1)}, f32[3,2048]{1,0:T(4,128)S(1)}, u32[]{:S(2)}, u32[]{:S(2)}) collective-permute-start(f32[3,2048]{1,0:T(4,128)S(1)} %slice.189), channel_id=1, source_target_pairs={{0,4},{4,8},{8,12},{12,16},{16,20},{20,24},{24,28},{1,5},{5,9},{9,... | collective-permute-start | bytes 73736 | tf_op jit(solution)/shard_map/ppermute | solution.py:10
  23.8 6.6 %copy-start.2 = (f32[128,2048]{1,0:T(8,128)S(1)}, f32[128,2048]{1,0:T(8,128)}, u32[]{:S(2)}) copy-start(f32[128,2048]{1,0:T(8,128)} %param.7) | copy-start | bytes 3145732
  24.5 5.9 %collective-permute-start.2 = (f32[3,2048]{1,0:T(4,128)S(1)}, f32[3,2048]{1,0:T(4,128)S(1)}, u32[]{:S(2)}, u32[]{:S(2)}) collective-permute-start(f32[3,2048]{1,0:T(4,128)S(1)} %slice.194), channel_id=1, source_target_pairs={{0,4},{4,8},{8,12},{12,16},{16,20},{20,24},{24,28},{1,5},{5,9},{9,... | collective-permute-start | bytes 73736 | tf_op jit(solution)/shard_map/ppermute | solution.py:10
  31.9 7.0 %collective-permute-start.3 = (f32[3,2048]{1,0:T(4,128)S(1)}, f32[3,2048]{1,0:T(4,128)S(1)}, u32[]{:S(2)}, u32[]{:S(2)}) collective-permute-start(f32[3,2048]{1,0:T(4,128)S(1)} %slice.199), channel_id=1, source_target_pairs={{4,0},{8,4},{12,8},{16,12},{20,16},{24,20},{28,24},{5,1},{9,5},{13... | collective-permute-start | bytes 73736 | tf_op jit(solution)/shard_map/ppermute | solution.py:10
  40.6 2.6 %copy-start.1 = (f32[128,2048]{1,0:T(8,128)}, f32[128,2048]{1,0:T(8,128)S(1)}, u32[]{:S(2)}) copy-start(f32[128,2048]{1,0:T(8,128)S(1)} %get-tuple-element.30) | copy-start | bytes 3145732
  40.6 7.0 %collective-permute-start.4 = (f32[3,2048]{1,0:T(4,128)S(1)}, f32[3,2048]{1,0:T(4,128)S(1)}, u32[]{:S(2)}, u32[]{:S(2)}) collective-permute-start(f32[3,2048]{1,0:T(4,128)S(1)} %slice.204), channel_id=1, source_target_pairs={{4,0},{8,4},{12,8},{16,12},{20,16},{24,20},{28,24},{5,1},{9,5},{13... | collective-permute-start | bytes 73736 | tf_op jit(solution)/shard_map/ppermute | solution.py:10
  41.9 5.7 %copy-start = (f32[128,2048]{1,0:T(8,128)S(1)}, f32[128,2048]{1,0:T(8,128)}, u32[]{:S(2)}) copy-start(f32[128,2048]{1,0:T(8,128)} %param.4) | copy-start | bytes 3145732
  51.1 6.7 %collective-permute-start.5 = (f32[3,2048]{1,0:T(4,128)S(1)}, f32[3,2048]{1,0:T(4,128)S(1)}, u32[]{:S(2)}, u32[]{:S(2)}) collective-permute-start(f32[3,2048]{1,0:T(4,128)S(1)} %slice.209), channel_id=1, source_target_pairs={{4,0},{8,4},{12,8},{16,12},{20,16},{24,20},{28,24},{5,1},{9,5},{13... | collective-permute-start | bytes 73736 | tf_op jit(solution)/shard_map/ppermute | solution.py:10
Sparse Core Ops, SparseCore 0:
  53.3 73.7 all-reduce.1
where the time goes:
time: 138 us; the launch traced here: 137 us
  waiting for transfers between devices  85.6 us (62%)
  starting transfers between devices  16.9 us (12%)
  between operations  14.2 us (10%)
  other arithmetic  14.1 us (10%)
  local copies, waits for them, and re-layouts  6.21 us (4%)
    psum x1, waiting for transfers between devices, shards(): summed = lax.psum(all_terms, 'seq')  67.9 us
    ppermute x6, waiting for transfers between devices, passed_along(): return lax.ppermute(array, axis, pairs)  17.7 us
    ppermute x6, starting transfers between devices, passed_along(): return lax.ppermute(array, axis, pairs)  16.9 us
    mul x3, other arithmetic, shards(): act = preact * jax.nn.sigmoid(preact)  5.36 us
    reduce_sum x1, other arithmetic, shards(): jnp.sum(pre_grad * padded[offset:offset + shard_len], axis=0)  3.34 us
    reduce_sum x2, other arithmetic, shards(): term_list[layer] = jnp.stack(weight_terms + [jnp.sum(pre_grad, axis=0)])  3.17 us
  transfers between devices with their start and end apart: 7, of which 6 were waited for; matrix products, arithmetic and copies ran while one was open for 4% of the time, Pallas kernels for 0%

commit v1 on v0

v1 whole, which is shorter than its diff:
```python
import jax
import jax.numpy as jnp
from jax import lax
from jax.sharding import PartitionSpec as P


def passed_along(array, axis, by):
    devices = lax.axis_size(axis)
    pairs = [(i, i + by) for i in range(devices) if 0 <= i + by < devices]
    return lax.ppermute(array, axis, pairs)


def summed_over(array, axis):
    devices = lax.axis_size(axis)
    bit = 1
    while bit < devices:
        array = array + lax.ppermute(array, axis, [(i, i ^ bit) for i in range(devices)])
        bit *= 2
    return array


def shards(inputs, conv_weight, conv_bias, cotangent):
    n, width = inputs.shape
    layers, taps = conv_weight.shape[:2]
    reach = taps - 1
    halo = layers * reach
    packed = lambda a: a.reshape(a.shape[0], width // 128, 128)
    before = passed_along(packed(inputs[n - halo :]), "seq", 1).reshape(halo, width)
    after = passed_along(
        packed(jnp.concatenate([inputs[:halo], cotangent[:halo]], axis=0)), "seq", -1
    ).reshape(2 * halo, width)
    first = lax.axis_index("seq") == 0
    act = jnp.concatenate([before, inputs, after[:halo]], axis=0)
    grad = jnp.concatenate([cotangent, after[halo:]], axis=0)
    saved = []
    for layer in range(layers):
        rows = act.shape[0] - reach
        preact = conv_bias[layer][None, :] + sum(
            conv_weight[layer, k][None, :] * act[k : k + rows] for k in range(taps)
        )
        lead = halo - (layer + 1) * reach
        saved.append((act[lead : lead + reach + n], preact[lead:]))
        act = preact * jax.nn.sigmoid(preact)
        if lead:
            keep = jnp.logical_or(jnp.logical_not(first), jnp.arange(rows) >= lead)
            act = jnp.where(keep[:, None], act, 0.0)
    output = act[:n]
    terms = [None] * layers
    for layer in reversed(range(layers)):
        padded, preact = saved[layer]
        rows = grad.shape[0]
        gate = jax.nn.sigmoid(preact[:rows])
        pre_grad = grad * gate * (1.0 + preact[:rows] * (1.0 - gate))
        grad = sum(
            conv_weight[layer, k][None, :]
            * pre_grad[reach - k : reach - k + rows - reach]
            for k in range(taps)
        )
        own = pre_grad[:n]
        terms[layer] = jnp.stack(
            [jnp.sum(own * padded[k : k + n], axis=0) for k in range(taps)]
            + [jnp.sum(own, axis=0)]
        )
    total = summed_over(jnp.stack(terms).reshape(-1, 128), "seq")
    total = total.reshape(layers, taps + 1, width)
    return output, grad, total[:, :taps], total[:, taps]


def solution(mesh):
    in_specs = (P("seq", "chan"), P(None, None, "chan"), P(None, "chan"), P("seq", "chan"))
    out_specs = (P("seq", "chan"), P("seq", "chan"), P(None, None, "chan"), P(None, "chan"))
    return jax.shard_map(shards, mesh=mesh, in_specs=in_specs, out_specs=out_specs, check_vma=False)
```

time: 138 us -> 42.1 us (0.31)
  waiting for transfers between devices: 85.6 us -> 14.6 us
  between operations: 14.2 us -> 0.92 us
  other arithmetic: 14.1 us -> 9.03 us
  starting transfers between devices: 16.9 us -> 13.9 us
  local copies, waits for them, and re-layouts: 6.21 us -> 3.43 us
    psum x1 -> x0, waiting for transfers between devices: 67.9 us -> none  [shards(): summed = lax.psum(all_terms, 'seq')]
    ppermute x6 -> x2, waiting for transfers between devices: 17.7 us -> 5.68 us  [passed_along(): return lax.ppermute(array, axis, pairs)]
    ppermute x6 -> x2, starting transfers between devices: 16.9 us -> 6.33 us  [passed_along(): return lax.ppermute(array, axis, pairs)]
    ppermute x0 -> x3, waiting for transfers between devices: none -> 8.94 us  [summed_over(): lax.ppermute(array, axis, [(i, i ^ bit) for i in range(devices)])]
    ppermute x0 -> x3, starting transfers between devices: none -> 7.53 us  [summed_over(): lax.ppermute(array, axis, [(i, i ^ bit) for i in range(devices)])]
    mul x3 -> x1, other arithmetic: 5.36 us -> 1.08 us  [shards(): act = preact * jax.nn.sigmoid(preact)]
    reduce_sum x3, other arithmetic: 6.51 us -> 3.17 us  [shards(): jnp.sum(own * padded[k:k + n], axis=0)]
    mul x0 -> x3, other arithmetic: none -> 2.65 us  [shards(): pre_grad = grad * gate * (1.0 + preact[:rows] * (1.0 - gate))]
  transfers between devices with their start and end apart: 7 -> 5, of which waited for: 6 -> 5; matrix products, arithmetic and copies ran while one was open for 4% -> 4% of each run, Pallas kernels for 0% -> 0%
where the time goes in v1:
time: 42.1 us; the launch traced here: 41.9 us
  waiting for transfers between devices  14.6 us (35%)
  starting transfers between devices  13.9 us (33%)
  other arithmetic  9.03 us (21%)
  local copies, waits for them, and re-layouts  3.43 us (8%)
  between operations  0.92 us (2%)
    ppermute x3, waiting for transfers between devices, summed_over(): lax.ppermute(array, axis, [(i, i ^ bit) for i in range(devices)])  8.94 us
    ppermute x3, starting transfers between devices, summed_over(): lax.ppermute(array, axis, [(i, i ^ bit) for i in range(devices)])  7.53 us
    ppermute x2, starting transfers between devices, passed_along(): return lax.ppermute(array, axis, pairs)  6.33 us
    ppermute x2, waiting for transfers between devices, passed_along(): return lax.ppermute(array, axis, pairs)  5.68 us
    reduce_sum x3, other arithmetic, shards(): jnp.sum(own * padded[k:k + n], axis=0)  3.17 us
    mul x3, other arithmetic, shards(): pre_grad = grad * gate * (1.0 + preact[:rows] * (1.0 - gate))  2.65 us
    select_n x2, other arithmetic, shards(): act = jnp.where(keep[:, None], act, 0.0)  1.59 us
    unnamed x17, local copies, waits for them, and re-layouts  1.29 us
  transfers between devices with their start and end apart: 5, of which 5 were waited for; matrix products, arithmetic and copies ran while one was open for 4% of the time, Pallas kernels for 0%

profile of v1, /device:TPU:0, one launch (start us, length us, event | category | flops | bytes accessed | tf_op | source)
XLA Modules:
  0.0 41.9 jit_solution(13709547764642294091)
XLA Ops:
  0.6 0.0 slice-start
  0.6 0.0 copy-start.3
  0.7 0.0 copy-start.2
  0.7 1.0 %fusion.45 = (f32[9,2048]{1,0:T(8,128)S(1)}, f32[9,2048]{1,0:T(8,128)S(1)}) fusion(f32[128,2048]{1,0:T(8,128)} %param.4), kind=kLoop, calls=%fused_computation.93 | loop fusion | bytes 294912 | tf_op jit(solution)/shard_map/slice | solution.py:28
  1.8 4.9 %collective-permute-start = (f32[9,16,128]{2,1,0:T(8,128)S(1)}, f32[9,16,128]{2,1,0:T(8,128)S(1)}, u32[]{:S(2)}, u32[]{:S(2)}) collective-permute-start(f32[9,16,128]{2,1,0:T(8,128)S(1)} %slice.338), channel_id=1, source_target_pairs={{0,4},{4,8},{8,12},{12,16},{16,20},{20,24},{24,28},{1,5},{5,9},{9,... | collective-permute-start | bytes 221192 | tf_op jit(solution)/shard_map/ppermute | solution.py:10
  6.7 0.0 slice-done
  6.7 0.0 copy-start
  6.8 1.4 %collective-permute-start.1 = (f32[18,16,128]{2,1,0:T(8,128)S(1)}, f32[18,16,128]{2,1,0:T(8,128)S(1)}, u32[]{:S(2)}, u32[]{:S(2)}) collective-permute-start(f32[18,16,128]{2,1,0:T(8,128)S(1)} %slice.339), channel_id=1, source_target_pairs={{4,0},{8,4},{12,8},{16,12},{20,16},{24,20},{28,24},{5,1},{9,5},{13... | collective-permute-start | bytes 442376 | tf_op jit(solution)/shard_map/ppermute | solution.py:10
  8.2 0.0 copy-done.3
  8.3 0.0 copy-done.2
  8.3 0.1 fusion.47
  8.4 0.3 collective-permute-done
  8.7 5.4 %collective-permute-done.1 = f32[18,16,128]{2,1,0:T(8,128)S(1)} collective-permute-done((f32[18,16,128]{2,1,0:T(8,128)S(1)}, f32[18,16,128]{2,1,0:T(8,128)S(1)}, u32[]{:S(2)}, u32[]{:S(2)}) %collective-permute-start.1) | collective-permute-done | bytes 147488 | tf_op jit(solution)/shard_map/ppermute | solution.py:10
  14.3 0.0 copy-done
  14.3 0.1 pad_maximum_fusion
  14.4 0.8 %multiply_select_fusion.1 = (f32[143,2048]{1,0:T(8,128)S(1)}, f32[143,2048]{1,0:T(8,128)S(1)}) fusion(pred[143]{0:T(512)(128)(4,1)S(1)} %compare_or_fusion, f32[146,2048]{1,0:T(8,128)S(1)} %pad_maximum_fusion, f32[2048]{0:T(1024)S(1)} %bitcast.73, f32[2048]{0:T(1024)S(1)} %bitcast.75, f32[2048]{0:T(1024)S(1)} %bitcast.77, f32[2048]{0:T(1024)S(1)} %bitcast.79, ...), kind=kLoop, calls=%fused_computation.31 | loop fusion | flops 3807232 | bytes 7069839 | tf_op jit(solution)/shard_map/jit(_where)/select_n | solution.py:46
  15.2 0.0 copy-start.1
  15.2 0.8 %multiply_select_fusion = (f32[140,2048]{1,0:T(8,128)S(1)}, f32[140,2048]{1,0:T(8,128)S(1)}) fusion(pred[140]{0:T(512)(128)(4,1)S(1)} %compare_or_fusion.1, f32[143,2048]{1,0:T(8,128)S(1)} %get-tuple-element.27, f32[2048]{0:T(1024)S(1)} %bitcast.81, f32[2048]{0:T(1024)S(1)} %bitcast.83, f32[2048]{0:T(1024)S(1)} %bitcast.85, f32[2048]{0:T(1024)S(1)} %bitcast.87, ...), kind=kLoop, calls=%fused_computation.30 | loop fusion | flops 3727360 | bytes 6922380 | tf_op jit(solution)/shard_map/jit(_where)/select_n | solution.py:46
  16.0 0.4 copy-done.1
  16.4 0.9 %fusion.12 = (f32[137,2048]{1,0:T(8,128)S(1)}, f32[137,2048]{1,0:T(8,128)S(1)}) fusion(f32[9,2048]{1,0:T(8,128)S(1)} %bitcast.55, f32[128,2048]{1,0:T(8,128)S(1)} %copy-done.1, f32[140,2048]{1,0:T(8,128)S(1)} %get-tuple-element.25, f32[2048]{0:T(1024)S(1)} %bitcast.69, f32[2048]{0:T(1024)S(1)} %bitcast.71, f32[2048]{0:T(1024)S(1)} %bitcast.67, ...), kind=kLoop, calls=%fused_computation.28 | loop fusion | flops 4769792 | bytes 7897088 | tf_op jit(solution)/shard_map/mul | solution.py:53
  17.3 0.6 %fusion.29 = (f32[2048]{0:T(1024)S(1)}, f32[2048]{0:T(1024)S(1)}, f32[2048]{0:T(1024)S(1)}, f32[2048]{0:T(1024)S(1)}, f32[2048]{0:T(1024)S(1)}) fusion(f32[140,2048]{1,0:T(8,128)S(1)} %get-tuple-element.25, f32[137,2048]{1,0:T(8,128)S(1)} %get-tuple-element.23), kind=kLoop, calls=%fused_computation.59 | loop fusion | flops 2349056 | bytes 5283840 | tf_op jit(solution)/shard_map/reduce_sum | solution.py:61
  17.9 0.9 %fusion.20 = f32[134,2048]{1,0:T(8,128)S(1)} fusion(f32[137,2048]{1,0:T(8,128)S(1)} %get-tuple-element.23, f32[140,2048]{1,0:T(8,128)S(1)} %get-tuple-element.26, f32[2048]{0:T(1024)S(1)} %bitcast.70, f32[2048]{0:T(1024)S(1)} %bitcast.72, f32[2048]{0:T(1024)S(1)} %bitcast.68, f32[2048]{0:T(1024)S(1)} %bitcast.66), kind=kLoop, calls=%fused_computation.46 | loop fusion | flops 4116480 | bytes 6619136 | tf_op jit(solution)/shard_map/mul | solution.py:53
  18.8 0.6 %fusion.33 = (f32[2048]{0:T(1024)S(1)}, f32[2048]{0:T(1024)S(1)}, f32[2048]{0:T(1024)S(1)}, f32[2048]{0:T(1024)S(1)}, f32[2048]{0:T(1024)S(1)}) fusion(f32[143,2048]{1,0:T(8,128)S(1)} %get-tuple-element.27, f32[134,2048]{1,0:T(8,128)S(1)} %fusion.20), kind=kLoop, calls=%fused_computation.67 | loop fusion | flops 2349056 | bytes 5283840 | tf_op jit(solution)/shard_map/reduce_sum | solution.py:61
  19.4 0.9 %fusion.15 = f32[131,2048]{1,0:T(8,128)S(1)} fusion(f32[134,2048]{1,0:T(8,128)S(1)} %fusion.20, f32[143,2048]{1,0:T(8,128)S(1)} %get-tuple-element.28, f32[2048]{0:T(1024)S(1)} %bitcast.82, f32[2048]{0:T(1024)S(1)} %bitcast.84, f32[2048]{0:T(1024)S(1)} %bitcast.86, f32[2048]{0:T(1024)S(1)} %bitcast.88), kind=kLoop, calls=%fused_computation.37 | loop fusion | flops 4024320 | bytes 6471680 | tf_op jit(solution)/shard_map/mul | solution.py:53
  20.3 1.9 %fusion.38 = (f32[2048]{0:T(1024)S(1)}, f32[2048]{0:T(1024)S(1)}, f32[2048]{0:T(1024)S(1)}, f32[2048]{0:T(1024)S(1)}, f32[2048]{0:T(1024)S(1)}, /*index=5*/f32[128,2048]{1,0:T(8,128)}) fusion(f32[128,2048]{1,0:T(8,128)S(1)} %copy-done, f32[9,2048]{1,0:T(8,128)S(1)} %bitcast.52, f32[131,2048]{1,0:T(8,128)S(1)} %fusion.15, f32[2048]{0:T(1024)S(1)} %bitcast.74, ...), kind=kLoop, calls=%fused_computation.76 | loop fusion | flops 4970496 | bytes 6438912 | tf_op jit(solution)/shard_map/reduce_sum | solution.py:61
  22.3 0.1 stack.85
  22.3 0.1 stack.78
  22.4 0.1 stack.71
  22.6 2.5 %collective-permute-start.2 = (f32[240,128]{1,0:T(8,128)S(1)}, f32[240,128]{1,0:T(8,128)S(1)}, u32[]{:S(2)}, u32[]{:S(2)}) collective-permute-start(f32[240,128]{1,0:T(8,128)S(1)} %reshape.51), channel_id=1, source_target_pairs={{0,4},{4,0},{8,12},{12,8},{16,20},{20,16},{24,28},{28,24},{1,5},{5... | collective-permute-start | bytes 368648 | tf_op jit(solution)/shard_map/ppermute | solution.py:17
  25.1 2.9 %collective-permute-done.2 = f32[240,128]{1,0:T(8,128)S(1)} collective-permute-done((f32[240,128]{1,0:T(8,128)S(1)}, f32[240,128]{1,0:T(8,128)S(1)}, u32[]{:S(2)}, u32[]{:S(2)}) %collective-permute-start.2) | collective-permute-done | bytes 122912 | tf_op jit(solution)/shard_map/ppermute | solution.py:17
  27.9 1.6 %collective-permute-start.3 = (f32[240,128]{1,0:T(8,128)S(1)}, f32[240,128]{1,0:T(8,128)S(1)}, u32[]{:S(2)}, u32[]{:S(2)}) collective-permute-start(f32[240,128]{1,0:T(8,128)S(1)} %add.153), channel_id=1, source_target_pairs={{0,8},{4,12},{8,0},{12,4},{16,24},{20,28},{24,16},{28,20},{1,9},{5... | collective-permute-start | bytes 368648 | tf_op jit(solution)/shard_map/ppermute | solution.py:17
  29.6 0.3 add_divide_fusion
  29.9 3.0 %collective-permute-done.3 = f32[240,128]{1,0:T(8,128)S(1)} collective-permute-done((f32[240,128]{1,0:T(8,128)S(1)}, f32[240,128]{1,0:T(8,128)S(1)}, u32[]{:S(2)}, u32[]{:S(2)}) %collective-permute-start.3) | collective-permute-done | bytes 122912 | tf_op jit(solution)/shard_map/ppermute | solution.py:17
  32.9 3.4 %collective-permute-start.4 = (f32[240,128]{1,0:T(8,128)S(1)}, f32[240,128]{1,0:T(8,128)S(1)}, u32[]{:S(2)}, u32[]{:S(2)}) collective-permute-start(f32[240,128]{1,0:T(8,128)S(1)} %add.154), channel_id=1, source_target_pairs={{0,16},{4,20},{8,24},{12,28},{16,0},{20,4},{24,8},{28,12},{1,17},{... | collective-permute-start | bytes 368648 | tf_op jit(solution)/shard_map/ppermute | solution.py:17
  36.3 1.1 %slice_multiply_fusion.31 = f32[128,2048]{1,0:T(8,128)} fusion(f32[137,2048]{1,0:T(8,128)S(1)} %add_divide_fusion, f32[137,2048]{1,0:T(8,128)S(1)} %get-tuple-element.24), kind=kLoop, calls=%fused_computation.83 | loop fusion | flops 262144 | bytes 3145728 | tf_op jit(solution)/shard_map/mul | solution.py:43
  37.4 3.1 %collective-permute-done.4 = f32[240,128]{1,0:T(8,128)S(1)} collective-permute-done((f32[240,128]{1,0:T(8,128)S(1)}, f32[240,128]{1,0:T(8,128)S(1)}, u32[]{:S(2)}, u32[]{:S(2)}) %collective-permute-start.4) | collective-permute-done | bytes 122912 | tf_op jit(solution)/shard_map/ppermute | solution.py:17
  40.6 0.7 %slice.336 = f32[3,4,2048]{2,1,0:T(4,128)} slice(f32[3,5,2048]{2,1,0:T(8,128)S(1)} %reshape.52), slice={[0:3], [0:4], [0:2048]} | slice | bytes 196608 | tf_op jit(solution)/shard_map/slice | solution.py:66
  41.2 0.6 %copy.16 = f32[3,1,2048]{2,0,1:T(4,128)} copy(f32[3,1,2048]{2,1,0:T(1,128)S(1)} %slice.337) | data formatting | bytes 49152
  (22 shorter events, 0.5 us)
Async XLA Ops:
  0.6 6.0 %slice-start = ((f32[128,2048]{1,0:T(8,128)}), f32[9,2048]{1,0:T(8,128)S(1)}, s32[]{:S(2)}) async-start(f32[128,2048]{1,0:T(8,128)} %param.7), calls=%async_computation | async-start | bytes 262144 | tf_op jit(solution)/shard_map/slice | solution.py:30
  0.6 7.6 %copy-start.3 = (f32[3,2048]{1,0:T(4,128)S(1)}, f32[3,2048]{1,0:T(4,128)}, u32[]{:S(2)}) copy-start(f32[3,2048]{1,0:T(4,128)} %param.6) | copy-start | bytes 73732
  0.7 7.6 %copy-start.2 = (f32[3,4,2048]{2,1,0:T(4,128)S(1)}, f32[3,4,2048]{2,1,0:T(4,128)}, u32[]{:S(2)}) copy-start(f32[3,4,2048]{2,1,0:T(4,128)} %param.5) | copy-start | bytes 294916
  1.8 6.9 %collective-permute-start = (f32[9,16,128]{2,1,0:T(8,128)S(1)}, f32[9,16,128]{2,1,0:T(8,128)S(1)}, u32[]{:S(2)}, u32[]{:S(2)}) collective-permute-start(f32[9,16,128]{2,1,0:T(8,128)S(1)} %slice.338), channel_id=1, source_target_pairs={{0,4},{4,8},{8,12},{12,16},{16,20},{20,24},{24,28},{1,5},{5,9},{9,... | collective-permute-start | bytes 221192 | tf_op jit(solution)/shard_map/ppermute | solution.py:10
  6.7 7.5 %copy-start = (f32[128,2048]{1,0:T(8,128)S(1)}, f32[128,2048]{1,0:T(8,128)}, u32[]{:S(2)}) copy-start(f32[128,2048]{1,0:T(8,128)} %param.4) | copy-start | bytes 3145732
  6.8 7.3 %collective-permute-start.1 = (f32[18,16,128]{2,1,0:T(8,128)S(1)}, f32[18,16,128]{2,1,0:T(8,128)S(1)}, u32[]{:S(2)}, u32[]{:S(2)}) collective-permute-start(f32[18,16,128]{2,1,0:T(8,128)S(1)} %slice.339), channel_id=1, source_target_pairs={{4,0},{8,4},{12,8},{16,12},{20,16},{24,20},{28,24},{5,1},{9,5},{13... | collective-permute-start | bytes 442376 | tf_op jit(solution)/shard_map/ppermute | solution.py:10
  15.2 1.2 %copy-start.1 = (f32[128,2048]{1,0:T(8,128)S(1)}, f32[128,2048]{1,0:T(8,128)}, u32[]{:S(2)}) copy-start(f32[128,2048]{1,0:T(8,128)} %param.7) | copy-start | bytes 3145732
  22.6 5.3 %collective-permute-start.2 = (f32[240,128]{1,0:T(8,128)S(1)}, f32[240,128]{1,0:T(8,128)S(1)}, u32[]{:S(2)}, u32[]{:S(2)}) collective-permute-start(f32[240,128]{1,0:T(8,128)S(1)} %reshape.51), channel_id=1, source_target_pairs={{0,4},{4,0},{8,12},{12,8},{16,20},{20,16},{24,28},{28,24},{1,5},{5... | collective-permute-start | bytes 368648 | tf_op jit(solution)/shard_map/ppermute | solution.py:17
  27.9 4.9 %collective-permute-start.3 = (f32[240,128]{1,0:T(8,128)S(1)}, f32[240,128]{1,0:T(8,128)S(1)}, u32[]{:S(2)}, u32[]{:S(2)}) collective-permute-start(f32[240,128]{1,0:T(8,128)S(1)} %add.153), channel_id=1, source_target_pairs={{0,8},{4,12},{8,0},{12,4},{16,24},{20,28},{24,16},{28,20},{1,9},{5... | collective-permute-start | bytes 368648 | tf_op jit(solution)/shard_map/ppermute | solution.py:17
  32.9 7.6 %collective-permute-start.4 = (f32[240,128]{1,0:T(8,128)S(1)}, f32[240,128]{1,0:T(8,128)S(1)}, u32[]{:S(2)}, u32[]{:S(2)}) collective-permute-start(f32[240,128]{1,0:T(8,128)S(1)} %add.154), channel_id=1, source_target_pairs={{0,16},{4,20},{8,24},{12,28},{16,0},{20,4},{24,8},{28,12},{1,17},{... | collective-permute-start | bytes 368648 | tf_op jit(solution)/shard_map/ppermute | solution.py:17
